TPU v7x, 32 devices: a whole 2x2x4 slice. The times are simulated.
32 devices in a mesh: obs: 2 (over y), bt: 4 (over z), freq: 2 (over x), pol: 2 (over core).
Axes of the slice: x: 2, y: 2, z: 4, core: 2. Of those that a mesh axis runs over, the one named last changes fastest.
Arguments:
- gains: float32 [16, 4, 8, 1984], P(('obs', 'bt', 'pol'), 'freq'), parts along dimension 0, may hold values from -3 to 3
- visibilities: bfloat16 [16, 4, 8, 4096], P('obs', 'freq', None, ('bt', 'pol')), parts along dimension 0, may hold values from -6 to 6
- first_station: int32 [8192], P(('obs', 'bt', 'pol')), parts along dimension 0, may hold values from 0 to 61
- second_station: int32 [8192], P(('obs', 'bt', 'pol')), parts along dimension 0, may hold values from 0 to 61, as said below
- filled_row_count: int32 [16], P(('obs', 'bt', 'pol')), parts along dimension 0, may hold values from 256 to 512
- facet_dir: int32 [16], P('obs'), parts along dimension 0, may hold values from 0 to 7, each once
Outputs:
- corrected: bfloat16 [16, 4, 8, 4096], P('obs', 'freq', None, ('bt', 'pol')), parts along dimension 0
There are 2 independent parts, one for each index of `obs`. A program takes and returns all parts, laid end to end along the dimension named above; each array names one. Nothing has to cross between parts.
Inputs may be any that keep to these rules, and one draw needn't show every extreme that they name: In every row second_station differs from first_station. `facet_dir`: each direction names exactly one facet.
All inputs are finite; a program needn't handle non-finite values.
Results may differ from a plain program's by a relative error of at most 0.001.
Values sent between devices are 32-bit elements; how exact they have to be, the bound alone decides.
A program may use at most 64 MiB of HBM per device.

v0:
```python
import jax
import jax.numpy as jnp
from jax import lax
from jax.sharding import PartitionSpec as P

ARRAY_STATIONS = 62
GAIN_SLOT_COUNT = 4


def entry(values, row_at, col_at):
    return (values[..., 2 * row_at + col_at, :], values[..., 4 + 2 * row_at + col_at, :])


def apply_jones(left_matrix, data, right_matrix):
    real_parts = []
    imag_parts = []
    for out_row in (0, 1):
        for out_col in (0, 1):
            total_re = jnp.zeros_like(left_matrix[..., 0, :])
            total_im = jnp.zeros_like(left_matrix[..., 0, :])
            for middle in (0, 1):
                for column in (0, 1):
                    left_re, left_im = entry(left_matrix, out_row, middle)
                    data_re, data_im = entry(data, middle, column)
                    right_re, right_im = entry(right_matrix, out_col, column)
                    prod_re = left_re * data_re - left_im * data_im
                    prod_im = left_re * data_im + left_im * data_re
                    total_re = total_re + prod_re * right_re + prod_im * right_im
                    total_im = total_im + prod_im * right_re - prod_re * right_im
            real_parts.append(total_re)
            imag_parts.append(total_im)
    return jnp.stack(real_parts + imag_parts, axis=-2)


def expand_slots(gain_window, antenna, block_rows, slots, stations):
    facets, chans, comps, _ = gain_window.shape
    current = gain_window[..., : slots * stations].reshape(facets, chans, comps, slots, stations)
    following = gain_window[..., stations:].reshape(facets, chans, comps, slots, stations)
    paired = jnp.concatenate([current, following], axis=4)
    per_slot = block_rows // slots
    grouped = antenna.reshape(slots, per_slot)
    fraction = (jnp.arange(per_slot, dtype=jnp.int32).astype(jnp.float32) + 0.5) / per_slot
    station_ids = jnp.arange(stations, dtype=jnp.int32)
    station_mask = (station_ids[None, :, None] == grouped[:, None, :]).astype(jnp.float32)
    table = jnp.concatenate([station_mask * (1.0 - fraction), station_mask * fraction], axis=1)
    spread = jnp.einsum("fckjn,jnp->fckjp", paired, table, precision=lax.Precision.HIGHEST)
    return spread.reshape(facets, chans, comps, block_rows)


def apply_correction(
    gain_window, block_visibilities, first_station_gain, second_station_gain, filled_rows
):
    block_rows = block_visibilities.shape[3]
    left_matrix = expand_slots(
        gain_window, first_station_gain, block_rows, GAIN_SLOT_COUNT, ARRAY_STATIONS
    )
    right_matrix = expand_slots(
        gain_window, second_station_gain, block_rows, GAIN_SLOT_COUNT, ARRAY_STATIONS
    )
    product = apply_jones(left_matrix, block_visibilities.astype(jnp.float32), right_matrix)
    live_mask = jnp.arange(block_rows, dtype=jnp.int32) < filled_rows
    return jnp.where(live_mask, product, 0.0 * product).astype(jnp.bfloat16)


def relay(payload):
    relaid = lax.all_to_all(payload, ("bt", "pol"), split_axis=3, concat_axis=0, tiled=True)
    return relaid


def select_facets(relaid, facet_dir):
    directions = relaid.shape[0]
    onehot = (facet_dir[:, None] == jnp.arange(directions, dtype=jnp.int32)[None, :]).astype(
        jnp.float32
    )
    return jnp.einsum("fd,dckn->fckn", onehot, relaid, precision=lax.Precision.HIGHEST)


def shards(gains, visibilities, first_station, second_station, filled_row_count, facet_dir):
    block_count = lax.axis_size(("bt", "pol"))
    dirs_here, chans_here, comps, _ = gains.shape
    by_slot = gains.reshape(
        dirs_here, chans_here, comps, block_count, GAIN_SLOT_COUNT, ARRAY_STATIONS
    )
    firsts = by_slot[:, :, :, :, 0, :]
    final_one = by_slot[:, :, :, block_count - 1 :, GAIN_SLOT_COUNT - 1, :]
    nexts = jnp.concatenate([firsts[:, :, :, 1:, :], final_one], axis=3)
    own_slots = by_slot.reshape(
        dirs_here, chans_here, comps, block_count, GAIN_SLOT_COUNT * ARRAY_STATIONS
    )
    windows = jnp.concatenate([own_slots, nexts], axis=4)
    windows = windows.reshape(
        dirs_here, chans_here, comps, block_count * (GAIN_SLOT_COUNT + 1) * ARRAY_STATIONS
    )
    gain_window = select_facets(relay(windows), facet_dir)
    return apply_correction(
        gain_window, visibilities, first_station, second_station, filled_row_count[0]
    )


def solution(mesh):
    return jax.shard_map(
        shards,
        mesh=mesh,
        in_specs=(
            P(("obs", "bt", "pol"), "freq", None, None),
            P("obs", "freq", None, ("bt", "pol")),
            P(("obs", "bt", "pol")),
            P(("obs", "bt", "pol")),
            P(("obs", "bt", "pol")),
            P("obs"),
        ),
        out_specs=P("obs", "freq", None, ("bt", "pol")),
        check_vma=False,
    )
```

profile of v0, /device:TPU:0, one launch (start us, length us, event | category | flops | bytes accessed | tf_op | source)
XLA Modules:
  0.0 31.5 jit_solution(10585168810742284929)
XLA Ops:
  0.0 1.3 %reshape.32 = f32[1,2,8,8,4,62]{5,4,3,2,1,0:T(4,128)S(1)} reshape(f32[1,2,8,1984]{3,2,1,0:T(8,128)} %param.6) | data formatting | bytes 253952 | tf_op jit(solution)/shard_map/reshape | solution.py:81
  1.4 1.0 %reshape_reshape.3 = f32[1,2,8,8,248]{4,3,2,1,0:T(8,128)S(1)} reshape(f32[1,2,8,1984]{3,2,1,0:T(8,128)} %param.6) | data formatting | bytes 253952 | tf_op jit(solution)/shard_map/reshape;reshape | solution.py:87
  2.4 0.1 maximum_maximum_fusion
  2.6 0.0 copy-start
  2.6 0.0 copy-start.1
  2.6 0.0 copy-start.2
  2.6 2.2 %copy.38 = f32[1,2,8,8,310]{2,1,4,3,0:T(2,128)S(1)} copy(f32[1,2,8,8,310]{4,3,2,1,0:T(8,128)S(1)} %maximum_maximum_fusion) | data formatting | bytes 317440 | tf_op jit(solution)/shard_map/concatenate | solution.py:90
  4.8 4.0 %reshape.41 = f32[8,1,4960]{2,1,0:T(1,128)} reshape(f32[2480,1,2,8]{3,2,1,0:T(2,128)S(1)} %bitcast.55) | data formatting | bytes 317440
  8.8 6.4 %all-to-all-start = ((f32[8,1,4960]{2,1,0:T(1,128)}), f32[8,1,4960]{2,1,0:T(1,128)S(1)}, u32[]{:S(2)}, u32[]{:S(2)}) async-start(f32[8,1,4960]{2,1,0:T(1,128)} %reshape.41), calls=%async_computation | async-start | bytes 319488 | tf_op jit(solution)/shard_map/all_to_all | solution.py:66
  15.1 0.0 copy-done
  15.2 0.1 copy_convert_fusion
  15.9 0.0 copy-done.1
  15.9 0.0 copy-done.2
  16.0 6.3 %all-to-all-done = f32[8,1,4960]{2,1,0:T(1,128)S(1)} async-done(((f32[8,1,4960]{2,1,0:T(1,128)}), f32[8,1,4960]{2,1,0:T(1,128)S(1)}, u32[]{:S(2)}, u32[]{:S(2)}) %all-to-all-start) | async-done | bytes 158752 | tf_op jit(solution)/shard_map/all_to_all | solution.py:66
  22.3 0.5 %broadcast.50 = f32[]{:T(128)} broadcast(f32[]{:T(128)} %constant.71), dimensions={} | broadcast | bytes 8 | tf_op jit(solution)/shard_map/all_to_all | solution.py:66
  22.8 1.0 %reduce = f32[8,4960]{1,0:T(8,128)S(1)} reduce(f32[8,1,4960]{2,1,0:T(1,128)S(1)} %all-to-all-done, f32[]{:T(128)} %broadcast.50), dimensions={1}, to_apply=%all_to_all.13.reduce_sub_computation | reduce | bytes 317444 | tf_op jit(solution)/shard_map/all_to_all | solution.py:66
  23.8 0.0 copy-start.3
  23.8 2.0 %reshape.42 = f32[2480,1,2,8]{3,2,1,0:T(2,128)S(1)} reshape(f32[8,4960]{1,0:T(8,128)S(1)} %reduce) | data formatting | bytes 317440
  25.8 2.1 %copy.65 = f32[1,2,8,8,310]{4,3,2,1,0:T(8,128)S(1)} copy(f32[1,2,8,8,310]{2,1,4,3,0:T(2,128)S(1)} %bitcast.56) | data formatting | bytes 317440 | tf_op jit(solution)/shard_map/all_to_all | solution.py:66
  27.9 0.3 fusion.5
  28.2 0.1 fusion.18
  28.3 0.2 reshape.34
  28.5 0.2 copy.40
  28.6 0.2 reshape.35
  28.8 0.2 copy.41
  29.0 0.4 %convolution_bitcast_fusion = f32[8,2,8,4,128]{4,2,1,0,3:T(8,128)S(1)} fusion(f32[4,62,128]{2,1,0:T(8,128)S(1)} %get-tuple-element.44, f32[4,62,128]{2,1,0:T(8,128)S(1)} %get-tuple-element.43, f32[8,2,8,4,62]{4,2,1,0,3:T(8,128)S(1)} %copy.41, f32[8,2,8,4,62]{4,2,1,0,3:T(8,128)S(1)} %copy.40), kind=kOutput, calls=%fused_computation | convolution fusion | flops 97644544 | bytes 770048 | tf_op jit(solution)/shard_map/fckjn,jnp->fckjp/dot_general | solution.py:46
  29.5 0.2 fusion.17
  29.6 0.4 %convolution_bitcast_fusion.1 = f32[8,2,8,4,128]{4,2,1,0,3:T(8,128)S(1)} fusion(f32[4,62,128]{2,1,0:T(8,128)S(1)} %get-tuple-element.45, f32[4,62,128]{2,1,0:T(8,128)S(1)} %get-tuple-element.46, f32[8,2,8,4,62]{4,2,1,0,3:T(8,128)S(1)} %copy.41, f32[8,2,8,4,62]{4,2,1,0,3:T(8,128)S(1)} %copy.40), kind=kOutput, calls=%fused_computation.1 | convolution fusion | flops 97644544 | bytes 770048 | tf_op jit(solution)/shard_map/fckjn,jnp->fckjp/dot_general | solution.py:46
  30.1 0.2 fusion.16
  30.3 0.1 add_dynamic-update-slice_fusion.3
  30.4 0.1 add_dynamic-update-slice_fusion.1
  30.8 0.7 %copy.61 = bf16[8,2,8,512]{3,2,1,0:T(8,128)(2,1)} copy(bf16[8,2,8,512]{3,0,2,1:T(8,128)(2,1)S(1)} %fusion) | data formatting | bytes 262144 | tf_op jit(solution)/shard_map/convert_element_type | solution.py:62
  (16 shorter events, 0.5 us)
Async XLA Ops:
  2.6 12.6 %copy-start = (bf16[8,2,8,512]{3,2,1,0:T(8,128)(2,1)S(1)}, bf16[8,2,8,512]{3,2,1,0:T(8,128)(2,1)}, u32[]{:S(2)}) copy-start(bf16[8,2,8,512]{3,2,1,0:T(8,128)(2,1)} %param.7) | copy-start | bytes 393220
  2.6 13.3 %copy-start.1 = (s32[512]{0:T(512)S(1)}, s32[512]{0:T(512)}, u32[]{:S(2)}) copy-start(s32[512]{0:T(512)} %param.9) | copy-start | bytes 6148
  2.6 13.3 %copy-start.2 = (s32[512]{0:T(512)S(1)}, s32[512]{0:T(512)}, u32[]{:S(2)}) copy-start(s32[512]{0:T(512)} %param.8) | copy-start | bytes 6148
  8.8 13.5 %all-to-all-start = ((f32[8,1,4960]{2,1,0:T(1,128)}), f32[8,1,4960]{2,1,0:T(1,128)S(1)}, u32[]{:S(2)}, u32[]{:S(2)}) async-start(f32[8,1,4960]{2,1,0:T(1,128)} %reshape.41), calls=%async_computation | async-start | bytes 319488 | tf_op jit(solution)/shard_map/all_to_all | solution.py:66
  23.8 4.1 %copy-start.3 = (s32[8]{0:T(128)S(1)}, s32[8]{0:T(128)}, u32[]{:S(2)}) copy-start(s32[8]{0:T(128)} %param.11) | copy-start | bytes 100
where the time goes:
time: 31.8 us; the launch traced here: 31.5 us
  local copies, waits for them, and re-layouts  15 us (47%)
  starting transfers between devices  6.35 us (20%)
  waiting for transfers between devices  6.29 us (20%)
  other arithmetic  1.77 us (6%)
  matrix products  1.16 us (4%)
  between operations  0.94 us (3%)
    all_to_all x1, starting transfers between devices, relay(): lax.all_to_all(payload, ('bt', 'pol'), split_axis=3, concat_axis=0, tiled...  6.35 us
    all_to_all x1, waiting for transfers between devices, relay(): lax.all_to_all(payload, ('bt', 'pol'), split_axis=3, concat_axis=0, tiled...  6.29 us
    unnamed x10, local copies, waits for them, and re-layouts  5.99 us
    all_to_all x2, local copies, waits for them, and re-layouts, relay(): lax.all_to_all(payload, ('bt', 'pol'), split_axis=3, concat_axis=0, tiled...  2.57 us
    concatenate x1, local copies, waits for them, and re-layouts, shards(): windows = jnp.concatenate([own_slots, nexts], axis=4)  2.18 us
    reshape x1, local copies, waits for them, and re-layouts, shards(): gains.reshape(dirs_here, chans_here, comps, block_count, GAIN_SLOT_COUNT,...  1.31 us
    another operation x1, local copies, waits for them, and re-layouts, shards(): by_slot.reshape(dirs_here, chans_here, comps, block_count, GAIN_SLOT_COUN...  1.03 us
    all_to_all x1, other arithmetic, relay(): lax.all_to_all(payload, ('bt', 'pol'), split_axis=3, concat_axis=0, tiled...  1.02 us
  transfers between devices with their start and end apart: 1, of which 1 were waited for; matrix products, arithmetic and copies ran while one was open for 0% of the time, Pallas kernels for 0%

commit v1 on v0

v1 whole, which is shorter than its diff:
```python
import functools

import jax
import jax.numpy as jnp
from jax import lax
from jax.experimental import pallas as pl
from jax.experimental.pallas import tpu as pltpu
from jax.sharding import PartitionSpec as P

ARRAY_STATIONS = 62
GAIN_SLOT_COUNT = 4
MESH = pl.DeviceIdType.MESH
LANES = 128
HALF = 64
COMPS = 8
F32 = jnp.float32
BF16 = jnp.bfloat16


def pair_tile(left, right):
    gap = jnp.zeros((left.shape[0], HALF - ARRAY_STATIONS), F32)
    return jnp.concatenate([left, gap, right, gap], axis=1)


def complex_dot(pairs, conj):
    re = im = None
    for (ar, ai), (br, bi) in pairs:
        if conj:
            pr = ar * br + ai * bi
            pi = ai * br - ar * bi
        else:
            pr = ar * br - ai * bi
            pi = ar * bi + ai * br
        re = pr if re is None else re + pr
        im = pi if im is None else im + pi
    return re, im


def jones(left, data, right):
    a = lambda m, i, j: (m[2 * i + j], m[4 + 2 * i + j])
    mid = {}
    for i in (0, 1):
        for j in (0, 1):
            mid[i, j] = complex_dot(
                [(a(left, i, t), a(data, t, j)) for t in (0, 1)], False
            )
    out = [None] * COMPS
    for i in (0, 1):
        for j in (0, 1):
            re, im = complex_dot(
                [(mid[i, t], a(right, j, t)) for t in (0, 1)], True
            )
            out[2 * i + j], out[4 + 2 * i + j] = re, im
    return out


def kernel(
    n,
    pols,
    gains_hbm,
    vis_hbm,
    first_hbm,
    second_hbm,
    filled_hbm,
    dir_hbm,
    out_ref,
    gains,
    vis,
    stations,
    filled,
    dirs,
    send,
    recv,
    table,
    planar,
    in_sem,
    send_sem,
    recv_sem,
):
    facets, chans, comps, rows = vis.shape
    slots = GAIN_SLOT_COUNT
    per_slot = rows // slots
    tiles = send.shape[1] // COMPS
    ck = chans * comps
    me = lax.axis_index("bt") * pols + lax.axis_index("pol")

    def where_is(block):
        return {"bt": block // pols, "pol": lax.rem(block, pols)}

    copies = [
        pltpu.make_async_copy(src, dst, in_sem.at[i])
        for i, (src, dst) in enumerate(
            [
                (gains_hbm, gains),
                (dir_hbm, dirs),
                (filled_hbm, filled),
                (first_hbm, stations.at[0]),
                (second_hbm, stations.at[1]),
                (vis_hbm, vis),
            ]
        )
    ]
    for copy in copies:
        copy.start()

    barrier = pltpu.get_barrier_semaphore()
    for off in range(1, n):
        pl.semaphore_signal(
            barrier,
            inc=1,
            device_id=where_is(lax.rem(me + off, n)),
            device_id_type=MESH,
        )

    copies[0].wait()
    lane = lax.broadcasted_iota(jnp.int32, (COMPS, LANES), 1)
    st = ARRAY_STATIONS

    def slot_of(c, t):
        t = min(t, n * slots - 1)
        return gains[0, c, :, t * st : (t + 1) * st]

    for b in range(n):
        at = 0
        for pair in range(slots // 2):
            for c in range(chans):
                t = b * slots + 2 * pair
                send[b, at * COMPS : (at + 1) * COMPS, :] = pair_tile(
                    slot_of(c, t), slot_of(c, t + 1)
                )
                at += 1
        for c in range(0, chans, 2):
            t = (b + 1) * slots
            send[b, at * COMPS : (at + 1) * COMPS, :] = pair_tile(
                slot_of(c, t), slot_of(min(c + 1, chans - 1), t)
            )
            at += 1

    pl.semaphore_wait(barrier, n - 1)
    slab = tiles * COMPS

    def remote(block, slot_dev):
        return pltpu.make_async_remote_copy(
            src_ref=send.at[block],
            dst_ref=recv.at[pl.ds(pl.multiple_of(slot_dev * slab, 8), slab), :],
            send_sem=send_sem.at[block],
            recv_sem=recv_sem.at[slot_dev],
            device_id=where_is(block),
            device_id_type=MESH,
        )

    order = sorted(range(1, n), key=lambda off: abs(off - n // 2))
    for off in order:
        remote(lax.rem(me + off, n), me).start()
    recv[pl.ds(pl.multiple_of(me * slab, 8), slab), :] = send[me]

    for copy in copies[1:5]:
        copy.wait()
    row = lax.broadcasted_iota(jnp.int32, (LANES, per_slot), 0)
    col = lax.broadcasted_iota(jnp.int32, (LANES, per_slot), 1)
    station = lax.rem(row, HALF)
    lower = row < HALF
    frac = (col.astype(F32) + 0.5) / per_slot
    live_rows = filled[0]
    for s in range(slots):
        now, then = 1.0 - frac, frac
        weight = jnp.where(lower, now, then) if s % 2 == 0 else jnp.where(lower, then, now)
        live = (col + s * per_slot) < live_rows
        first = stations[0, s : s + 1, :]
        second = stations[1, s : s + 1, :]
        lt = jnp.where((station == first) & live, weight, 0.0)
        rt = jnp.where(station == second, weight, 0.0)
        both = jnp.concatenate([lt, rt], axis=1).astype(BF16)
        table[s, 0:LANES, :] = both
        table[s, LANES : 2 * LANES, :] = both

    copies[5].wait()
    total = facets * ck
    prow = lax.broadcasted_iota(jnp.int32, (total, total), 0)
    pcol = lax.broadcasted_iota(jnp.int32, (total, total), 1)
    facet_of = pcol // ck
    dir_of = jnp.zeros_like(pcol)
    for f in range(facets):
        dir_of = jnp.where(facet_of == f, dirs[f], dir_of)
    target = lax.rem(pcol, ck) * facets + dir_of
    perm32 = jnp.where(prow == target, 1.0, 0.0)
    perm = perm32.astype(BF16)
    unperm = perm32.T.astype(BF16)
    flat = vis[...].astype(F32).reshape(total, rows).astype(BF16)
    planar[...] = jnp.dot(perm, flat, preferred_element_type=F32)

    for off in order:
        remote(me, lax.rem(me - off + n, n)).wait_recv()

    def gathered(at, c_rot):
        planes = []
        for k in range(comps):
            plane = recv[pl.ds(at * COMPS + k, facets, stride=slab), :]
            if c_rot:
                plane = pltpu.roll(plane, HALF, 1)
            planes.append(plane)
        return planes

    def stacked(pair):
        planes = []
        for c in range(chans):
            if pair < slots // 2:
                planes += gathered(pair * chans + c, False)
            else:
                planes += gathered((slots // 2) * chans + c // 2, c % 2 == 1)
        return jnp.concatenate(planes, axis=0)

    pairs = [stacked(p) for p in range(slots // 2 + 1)]
    in_low = lax.broadcasted_iota(jnp.int32, (total, LANES), 1) < HALF
    done = []
    for s in range(slots):
        made = []
        x = pairs[s // 2]
        if s % 2 == 1:
            x = jnp.where(in_low, pairs[s // 2 + 1], x)
        hi = x.astype(BF16)
        lo = (x - hi.astype(F32)).astype(BF16)
        spread = jnp.dot(
            jnp.concatenate([hi, lo], axis=1), table[s], preferred_element_type=F32
        )
        for c in range(chans):
            take = lambda k: slice((c * comps + k) * facets, (c * comps + k + 1) * facets)
            left = [spread[take(k), 0:per_slot] for k in range(comps)]
            right = [spread[take(k), per_slot:] for k in range(comps)]
            data = [planar[take(k), s * per_slot : (s + 1) * per_slot] for k in range(comps)]
            made += jones(left, data, right)
        done.append(jnp.concatenate(made, axis=0).astype(BF16))
        if s % 2 == 1:
            wide = jnp.concatenate(done, axis=1)
            done = []
            back = jnp.dot(unperm, wide, preferred_element_type=F32)
            for f in range(facets):
                for c in range(chans):
                    at = (f * chans + c) * comps
                    out_ref[f, c, :, (s - 1) * per_slot : (s + 1) * per_slot] = back[
                        at : at + comps, :
                    ].astype(BF16)

    for off in order:
        remote(lax.rem(me + off, n), me).wait_send()


def shards(gains, visibilities, first_station, second_station, filled_row_count, facet_dir):
    n = lax.axis_size(("bt", "pol"))
    pols = lax.axis_size("pol")
    facets, chans, comps, rows = visibilities.shape
    slots = GAIN_SLOT_COUNT
    tiles = (slots // 2) * chans + (chans + 1) // 2
    total = facets * chans * comps
    anywhere = pl.BlockSpec(memory_space=pl.ANY)
    return pl.pallas_call(
        functools.partial(kernel, n, pols),
        out_shape=jax.ShapeDtypeStruct(visibilities.shape, BF16),
        in_specs=[anywhere] * 6,
        out_specs=pl.BlockSpec(memory_space=pltpu.VMEM),
        scratch_shapes=[
            pltpu.VMEM(gains.shape, F32),
            pltpu.VMEM(visibilities.shape, BF16),
            pltpu.VMEM((2, slots, rows // slots), jnp.int32),
            pltpu.SMEM(filled_row_count.shape, jnp.int32),
            pltpu.SMEM(facet_dir.shape, jnp.int32),
            pltpu.VMEM((n, tiles * COMPS, LANES), F32),
            pltpu.VMEM((n * tiles * COMPS, LANES), F32),
            pltpu.VMEM((slots, 2 * LANES, 2 * (rows // slots)), BF16),
            pltpu.VMEM((total, rows), F32),
            pltpu.SemaphoreType.DMA((6,)),
            pltpu.SemaphoreType.DMA((n,)),
            pltpu.SemaphoreType.DMA((n,)),
        ],
        compiler_params=pltpu.CompilerParams(collective_id=0, has_side_effects=True),
        name="jones",
    )(
        gains,
        visibilities,
        first_station.reshape(slots, rows // slots),
        second_station.reshape(slots, rows // slots),
        filled_row_count,
        facet_dir,
    )


def solution(mesh):
    return jax.shard_map(
        shards,
        mesh=mesh,
        in_specs=(
            P(("obs", "bt", "pol"), "freq", None, None),
            P("obs", "freq", None, ("bt", "pol")),
            P(("obs", "bt", "pol")),
            P(("obs", "bt", "pol")),
            P(("obs", "bt", "pol")),
            P("obs"),
        ),
        out_specs=P("obs", "freq", None, ("bt", "pol")),
        check_vma=False,
    )
```

time: 31.8 us -> 13 us (0.41)
  local copies, waits for them, and re-layouts: 15 us -> 1.57 us
  Pallas kernels: 0 us -> 10.6 us
  starting transfers between devices: 6.35 us -> 0 us
  waiting for transfers between devices: 6.29 us -> 0 us
  other arithmetic: 1.77 us -> 0 us
  matrix products: 1.16 us -> 0 us
    pallas_call x0 -> x1, Pallas kernels: none -> 10.6 us  [shards(): pl.pallas_call(functools.partial(kernel, n, pols), out_shape=jax.ShapeDty...]
    all_to_all x1 -> x0, starting transfers between devices: 6.35 us -> none  [relay(): lax.all_to_all(payload, ('bt', 'pol'), split_axis=3, concat_axis=0, tiled...]
    all_to_all x1 -> x0, waiting for transfers between devices: 6.29 us -> none  [relay(): lax.all_to_all(payload, ('bt', 'pol'), split_axis=3, concat_axis=0, tiled...]
    unnamed x10 -> x1, local copies, waits for them, and re-layouts: 5.99 us -> 1.57 us
    all_to_all x2 -> x0, local copies, waits for them, and re-layouts: 2.57 us -> none  [relay(): lax.all_to_all(payload, ('bt', 'pol'), split_axis=3, concat_axis=0, tiled...]
    concatenate x1 -> x0, local copies, waits for them, and re-layouts: 2.18 us -> none  [shards(): windows = jnp.concatenate([own_slots, nexts], axis=4)]
    reshape x5 -> x0, local copies, waits for them, and re-layouts: 1.99 us -> none  [the longest x1 1.31 us: shards(): gains.reshape(dirs_here, chans_here, comps, block_count, GAIN_SLOT_COUNT,...]
    dot_general x3 -> x0, matrix products: 1.16 us -> none  [the longest x2 0.87 us: expand_slots(): jnp.einsum('fckjn,jnp->fckjp', paired, table, precision=lax.Precision.HIG...]
  transfers between devices with their start and end apart: 1 -> 0, of which waited for: 1 -> 0; matrix products, arithmetic and copies ran while one was open for 0% -> 0% of each run, Pallas kernels for 0% -> 0%
where the time goes in v1:
time: 13 us; the launch traced here: 12.9 us
  Pallas kernels  10.6 us (82%)
  local copies, waits for them, and re-layouts  1.57 us (12%)
  between operations  0.66 us (5%)
    pallas_call x1, Pallas kernels, shards(): pl.pallas_call(functools.partial(kernel, n, pols), out_shape=jax.ShapeDty...  10.6 us
    unnamed x1, local copies, waits for them, and re-layouts  1.57 us

profile of v1, /device:TPU:0, one launch (start us, length us, event | category | flops | bytes accessed | tf_op | source)
XLA Modules:
  0.0 12.9 jit_solution(4592245054562777107)
XLA Ops:
  0.7 10.6 %jones.1 = bf16[8,2,8,512]{3,2,1,0:T(8,128)(2,1)} custom-call(f32[1,2,8,1984]{3,2,1,0:T(8,128)} %gains_hbm.1, bf16[8,2,8,512]{3,2,1,0:T(8,128)(2,1)} %vis_hbm.1, s32[4,128]{1,0:T(4,128)} %bitcast.2, s32[4,128]{1,0:T(4,128)} %bitcast.3, s32[1]{0:T(128)S(6)} %copy.8.filled_hbm, s32[8]{0:T(128)} %dir_hbm.1), custom_call_target="tpu_custom_call" | custom-call | tf_op jit(solution)/shard_map/jones/pallas_call | solution.py:256
  11.3 1.6 %copy.9 = bf16[8,2,8,512]{3,2,1,0:T(8,128)(2,1)} copy(bf16[8,2,8,512]{3,2,1,0:T(8,128)(2,1)} %jones.1) | data formatting | bytes 262144

commit v2 on v1

--- a/solution.py
+++ b/solution.py
@@ -255,7 +255,7 @@
     anywhere = pl.BlockSpec(memory_space=pl.ANY)
     return pl.pallas_call(
         functools.partial(kernel, n, pols),
-        out_shape=jax.ShapeDtypeStruct(visibilities.shape, BF16),
+        out_shape=pltpu.VMEM(visibilities.shape, BF16),
         in_specs=[anywhere] * 6,
         out_specs=pl.BlockSpec(memory_space=pltpu.VMEM),
         scratch_shapes=[

time: 13 us -> 11.4 us (0.88)
  local copies, waits for them, and re-layouts: 1.57 us -> 0.66 us
  Pallas kernels: 10.6 us -> 9.99 us
    unnamed x1, local copies, waits for them, and re-layouts: 1.57 us -> 0.66 us
    pallas_call x1, Pallas kernels: 10.6 us -> 9.99 us  [shards(): pl.pallas_call(functools.partial(kernel, n, pols), out_shape=pltpu.VMEM(v...]
where the time goes in v2:
time: 11.4 us; the launch traced here: 11.3 us
  Pallas kernels  9.99 us (88%)
  local copies, waits for them, and re-layouts  0.66 us (6%)
  between operations  0.66 us (6%)
    pallas_call x1, Pallas kernels, shards(): pl.pallas_call(functools.partial(kernel, n, pols), out_shape=pltpu.VMEM(v...  9.99 us
    unnamed x1, local copies, waits for them, and re-layouts  0.66 us

profile of v2, /device:TPU:0, one launch (start us, length us, event | category | flops | bytes accessed | tf_op | source)
XLA Modules:
  0.0 11.3 jit_solution(2644713551937487081)
XLA Ops:
  0.7 10.0 %jones.1 = bf16[8,2,8,512]{3,2,1,0:T(8,128)(2,1)S(1)} custom-call(f32[1,2,8,1984]{3,2,1,0:T(8,128)} %gains_hbm.1, bf16[8,2,8,512]{3,2,1,0:T(8,128)(2,1)} %vis_hbm.1, s32[4,128]{1,0:T(4,128)} %bitcast.2, s32[4,128]{1,0:T(4,128)} %bitcast.3, s32[1]{0:T(128)S(6)} %copy.9.filled_hbm, s32[8]{0:T(128)} %dir_hbm.1), custom_call_target="tpu_custom_call" | custom-call | tf_op jit(solution)/shard_map/jones/pallas_call | solution.py:256
  10.6 0.7 %copy.8 = bf16[8,2,8,512]{3,2,1,0:T(8,128)(2,1)} copy(bf16[8,2,8,512]{3,2,1,0:T(8,128)(2,1)S(1)} %jones.1) | data formatting | bytes 262144

commit v3 on v2

--- a/solution.py
+++ b/solution.py
@@ -80,37 +80,36 @@
     facets, chans, comps, rows = vis.shape
     slots = GAIN_SLOT_COUNT
     per_slot = rows // slots
-    tiles = send.shape[1] // COMPS
+    tiles = send.shape[0] // COMPS // n
     ck = chans * comps
-    me = lax.axis_index("bt") * pols + lax.axis_index("pol")
-
-    def where_is(block):
-        return {"bt": block // pols, "pol": lax.rem(block, pols)}
+    bts = n // pols
+    my_bt, my_pol = lax.axis_index("bt"), lax.axis_index("pol")
+    me = my_bt * pols + my_pol
+    steps = [(dz, dp) for dz in range(bts) for dp in range(pols) if dz or dp]
+    steps.sort(key=lambda step: (step[0] == 0, abs(2 * step[0] - bts)))
+    peers = [
+        (lax.rem(my_bt + dz, bts), lax.rem(my_pol + dp, pols)) for dz, dp in steps
+    ]
 
     copies = [
         pltpu.make_async_copy(src, dst, in_sem.at[i])
-        for i, (src, dst) in enumerate(
-            [
-                (gains_hbm, gains),
-                (dir_hbm, dirs),
-                (filled_hbm, filled),
-                (first_hbm, stations.at[0]),
-                (second_hbm, stations.at[1]),
-                (vis_hbm, vis),
-            ]
+        for src, dst, i in [
+            (gains_hbm, gains, 0),
+            (first_hbm, stations.at[0], 1),
+            (second_hbm, stations.at[1], 1),
+            (dir_hbm, dirs, 2),
+            (filled_hbm, filled, 3),
+            (vis_hbm, vis, 4),
+        ]
+    ]
+    copies[0].start()
+    barrier = pltpu.get_barrier_semaphore()
+    for bt, pol in peers:
+        pl.semaphore_signal(
+            barrier, inc=1, device_id={"bt": bt, "pol": pol}, device_id_type=MESH
         )
-    ]
-    for copy in copies:
+    for copy in copies[1:]:
         copy.start()
-
-    barrier = pltpu.get_barrier_semaphore()
-    for off in range(1, n):
-        pl.semaphore_signal(
-            barrier,
-            inc=1,
-            device_id=where_is(lax.rem(me + off, n)),
-            device_id_type=MESH,
-        )
 
     copies[0].wait()
     lane = lax.broadcasted_iota(jnp.int32, (COMPS, LANES), 1)
@@ -125,13 +124,13 @@
         for pair in range(slots // 2):
             for c in range(chans):
                 t = b * slots + 2 * pair
-                send[b, at * COMPS : (at + 1) * COMPS, :] = pair_tile(
+                send[pl.ds((b * tiles + at) * COMPS, COMPS), :] = pair_tile(
                     slot_of(c, t), slot_of(c, t + 1)
                 )
                 at += 1
         for c in range(0, chans, 2):
             t = (b + 1) * slots
-            send[b, at * COMPS : (at + 1) * COMPS, :] = pair_tile(
+            send[pl.ds((b * tiles + at) * COMPS, COMPS), :] = pair_tile(
                 slot_of(c, t), slot_of(min(c + 1, chans - 1), t)
             )
             at += 1
@@ -139,23 +138,21 @@
     pl.semaphore_wait(barrier, n - 1)
     slab = tiles * COMPS
 
-    def remote(block, slot_dev):
-        return pltpu.make_async_remote_copy(
-            src_ref=send.at[block],
-            dst_ref=recv.at[pl.ds(pl.multiple_of(slot_dev * slab, 8), slab), :],
-            send_sem=send_sem.at[block],
-            recv_sem=recv_sem.at[slot_dev],
-            device_id=where_is(block),
+    mine = pl.ds(pl.multiple_of(me * slab, 8), slab)
+    for bt, pol in peers:
+        pltpu.make_async_remote_copy(
+            src_ref=send.at[pl.ds(pl.multiple_of((bt * pols + pol) * slab, 8), slab), :],
+            dst_ref=recv.at[mine, :],
+            send_sem=send_sem,
+            recv_sem=recv_sem,
+            device_id={"bt": bt, "pol": pol},
             device_id_type=MESH,
-        )
-
-    order = sorted(range(1, n), key=lambda off: abs(off - n // 2))
-    for off in order:
-        remote(lax.rem(me + off, n), me).start()
-    recv[pl.ds(pl.multiple_of(me * slab, 8), slab), :] = send[me]
-
-    for copy in copies[1:5]:
-        copy.wait()
+        ).start()
+    recv[mine, :] = send[mine, :]
+
+    pltpu.make_async_copy(stations, stations, in_sem.at[1]).wait()
+    copies[3].wait()
+    copies[4].wait()
     row = lax.broadcasted_iota(jnp.int32, (LANES, per_slot), 0)
     col = lax.broadcasted_iota(jnp.int32, (LANES, per_slot), 1)
     station = lax.rem(row, HALF)
@@ -189,8 +186,8 @@
     flat = vis[...].astype(F32).reshape(total, rows).astype(BF16)
     planar[...] = jnp.dot(perm, flat, preferred_element_type=F32)
 
-    for off in order:
-        remote(me, lax.rem(me - off + n, n)).wait_recv()
+    arrived = recv.at[pl.ds(0, (n - 1) * slab), :]
+    pltpu.make_async_copy(arrived, arrived, recv_sem).wait()
 
     def gathered(at, c_rot):
         planes = []
@@ -241,8 +238,8 @@
                         at : at + comps, :
                     ].astype(BF16)
 
-    for off in order:
-        remote(lax.rem(me + off, n), me).wait_send()
+    sent = send.at[pl.ds(0, (n - 1) * slab), :]
+    pltpu.make_async_copy(sent, sent, send_sem).wait()
 
 
 def shards(gains, visibilities, first_station, second_station, filled_row_count, facet_dir):
@@ -252,7 +249,7 @@
     slots = GAIN_SLOT_COUNT
     tiles = (slots // 2) * chans + (chans + 1) // 2
     total = facets * chans * comps
-    anywhere = pl.BlockSpec(memory_space=pl.ANY)
+    anywhere = pl.BlockSpec(memory_space=pltpu.HBM)
     return pl.pallas_call(
         functools.partial(kernel, n, pols),
         out_shape=pltpu.VMEM(visibilities.shape, BF16),
@@ -264,13 +261,13 @@
             pltpu.VMEM((2, slots, rows // slots), jnp.int32),
             pltpu.SMEM(filled_row_count.shape, jnp.int32),
             pltpu.SMEM(facet_dir.shape, jnp.int32),
-            pltpu.VMEM((n, tiles * COMPS, LANES), F32),
+            pltpu.VMEM((n * tiles * COMPS, LANES), F32),
             pltpu.VMEM((n * tiles * COMPS, LANES), F32),
             pltpu.VMEM((slots, 2 * LANES, 2 * (rows // slots)), BF16),
             pltpu.VMEM((total, rows), F32),
-            pltpu.SemaphoreType.DMA((6,)),
-            pltpu.SemaphoreType.DMA((n,)),
-            pltpu.SemaphoreType.DMA((n,)),
+            pltpu.SemaphoreType.DMA((5,)),
+            pltpu.SemaphoreType.DMA,
+            pltpu.SemaphoreType.DMA,
         ],
         compiler_params=pltpu.CompilerParams(collective_id=0, has_side_effects=True),
         name="jones",

time: 11.4 us -> 11.3 us (level)
  Pallas kernels: 9.99 us -> 9.82 us
    pallas_call x1, Pallas kernels: 9.99 us -> 9.82 us  [shards(): pl.pallas_call(functools.partial(kernel, n, pols), out_shape=pltpu.VMEM(v...]
where the time goes in v3:
time: 11.3 us; the launch traced here: 11.1 us
  Pallas kernels  9.82 us (87%)
  local copies, waits for them, and re-layouts  0.66 us (6%)
  between operations  0.66 us (6%)
    pallas_call x1, Pallas kernels, shards(): pl.pallas_call(functools.partial(kernel, n, pols), out_shape=pltpu.VMEM(v...  9.82 us
    unnamed x1, local copies, waits for them, and re-layouts  0.66 us

profile of v3, /device:TPU:0, one launch (start us, length us, event | category | flops | bytes accessed | tf_op | source)
XLA Modules:
  0.0 11.1 jit_solution(14578240336828323102)
XLA Ops:
  0.7 9.8 %jones.1 = bf16[8,2,8,512]{3,2,1,0:T(8,128)(2,1)S(1)} custom-call(f32[1,2,8,1984]{3,2,1,0:T(8,128)} %gains_hbm.1, bf16[8,2,8,512]{3,2,1,0:T(8,128)(2,1)} %vis_hbm.1, s32[4,128]{1,0:T(4,128)} %bitcast.2, s32[4,128]{1,0:T(4,128)} %bitcast.3, s32[1]{0:T(128)S(6)} %copy.9.filled_hbm, s32[8]{0:T(128)} %dir_hbm.1), custom_call_target="tpu_custom_call" | custom-call | tf_op jit(solution)/shard_map/jones/pallas_call | solution.py:253
  10.5 0.7 %copy.8 = bf16[8,2,8,512]{3,2,1,0:T(8,128)(2,1)} copy(bf16[8,2,8,512]{3,2,1,0:T(8,128)(2,1)S(1)} %jones.1) | data formatting | bytes 262144
